TPU v7x, 16 devices: a 4x2x1 block of a 4x4x8 slice. The times are simulated.
16 devices in a mesh: dp: 2 (over y, z), ep: 8 (over x, core).
Axes of the slice: x: 4, y: 2, z: 1, core: 2. Of those that a mesh axis runs over, the one named last changes fastest.
The devices are a block of a 4x4x8 slice.
Arguments:
- x_in: bfloat16 [1536, 2048], P(('dp', 'ep')), parts along dimension 0
- norm_gain: bfloat16 [2048], replicated
- w_router: bfloat16 [2048, 64], replicated
- expert_ids: int32 [1536, 8], P(('dp', 'ep')), parts along dimension 0
- w_gate: bfloat16 [64, 2048, 1024], P('ep')
- w_up: bfloat16 [64, 2048, 1024], P('ep')
- w_down: bfloat16 [64, 1024, 2048], P('ep')
Outputs:
- output: bfloat16 [1536, 2048], P(('dp', 'ep')), parts along dimension 0
There are 2 independent parts. A program takes and returns all parts, laid end to end along the dimension named above; an argument that names none is the same for every part.
All inputs are finite; a program needn't handle non-finite values.
Results may differ from a plain program's by a relative error of at most 0.00121.
Values are sent between devices in bfloat16 or wider.
A program may use at most 768 MiB of HBM per device.

v0:
```python
import jax
import jax.numpy as jnp
from jax import lax
from jax.sharding import PartitionSpec as P

EPS = 1e-6


def norm_and_gates(x_in, norm_gain, w_router, expert_ids):
    resid = x_in.astype(jnp.float32)
    mean_sq = jnp.mean(resid * resid, axis=-1, keepdims=True)
    normed = (resid * lax.rsqrt(mean_sq + EPS) * norm_gain.astype(jnp.float32)).astype(jnp.bfloat16)
    logits = jnp.dot(normed, w_router, preferred_element_type=jnp.float32)
    router_p = jax.nn.softmax(logits, axis=-1)
    picked = jnp.take_along_axis(router_p, expert_ids, axis=1)
    gates = picked / jnp.sum(picked, axis=1, keepdims=True)
    return resid, normed, gates


def route_slots(expert_ids, experts, capacity):
    flat_ids = expert_ids.reshape(-1)
    onehot = (flat_ids[:, None] == jnp.arange(experts, dtype=jnp.int32)[None, :]).astype(jnp.int32)
    before = jnp.cumsum(onehot, axis=0) - onehot
    position = jnp.sum(before * onehot, axis=1)
    return flat_ids * capacity + position


def expert_mlp(rows, w_gate, w_up, w_down):
    gate_val = jnp.einsum("erd,edf->erf", rows, w_gate, preferred_element_type=jnp.float32)
    up_val = jnp.einsum("erd,edf->erf", rows, w_up, preferred_element_type=jnp.float32)
    hidden_act = (jax.nn.silu(gate_val) * up_val).astype(jnp.bfloat16)
    return jnp.einsum("erf,efd->erd", hidden_act, w_down, preferred_element_type=jnp.float32).astype(jnp.bfloat16)


def solution(mesh):
    def local_block(x_in, norm_gain, w_router, expert_ids, w_gate, w_up, w_down):
        tokens, hidden = x_in.shape
        experts = w_router.shape[1]
        top_k = expert_ids.shape[1]
        capacity = 2 * tokens * top_k // experts
        resid, normed, gates = norm_and_gates(x_in, norm_gain, w_router, expert_ids)
        slots = route_slots(expert_ids, experts, capacity)
        choice_tok = jnp.arange(tokens * top_k, dtype=jnp.int32) // top_k
        slot_tok = jnp.full((experts * capacity,), tokens, jnp.int32).at[slots].set(choice_tok)
        outgoing = jnp.take(normed, slot_tok, axis=0, mode="fill", fill_value=0).reshape(experts, capacity, hidden)
        received = lax.all_to_all(outgoing, "ep", 0, 1, tiled=True)
        outputs = expert_mlp(received, w_gate, w_up, w_down)
        returned = lax.all_to_all(outputs, "ep", 1, 0, tiled=True).reshape(experts * capacity, hidden)
        y_sel = jnp.take(returned, slots, axis=0).reshape(tokens, top_k, hidden)
        mixed = jnp.sum(y_sel.astype(jnp.float32) * gates[:, :, None], axis=1)
        return (resid + mixed).astype(jnp.bfloat16)

    tok_spec = P(("dp", "ep"), None)
    expert_spec = P("ep", None, None)
    return jax.shard_map(local_block, mesh=mesh, in_specs=(tok_spec, P(None), P(None, None), tok_spec, expert_spec, expert_spec, expert_spec), out_specs=tok_spec, check_vma=False)
```

profile of v0, /device:TPU:113, one launch (start us, length us, event | category | flops | bytes accessed | tf_op | source)
XLA Modules:
  0.0 259.9 jit_solution(1696410687865263497)
XLA Ops:
  0.0 0.0 copy-start
  0.0 0.7 broadcast_multiply_fusion
  0.7 0.8 copy.34
  1.5 0.1 eq.26
  1.6 0.1 reshape.109
  1.7 0.1 copy.39
  1.8 0.1 mul.59
  1.9 1.8 reduce-window.6
  3.7 0.3 slice_reduce_fusion
  4.0 0.1 fusion.9
  4.2 3.4 %scatter_custom_fusion = s32[1536]{0:T(1024)S(1)} fusion(s32[768]{0:T(1024)S(1)} %fusion.18, s32[768]{0:T(1024)S(1)} %add_select_fusion, s32[]{:T(128)} %constant.70.clone.1), kind=kCustom, calls=%fused_computation.44 | custom fusion | bytes 6148 | tf_op jit(solution)/shard_map/scatter | solution.py:44
  7.6 1.2 fusion.3
  8.8 0.7 convert_element_type.31
  9.5 0.1 broadcast_in_dim.41
  9.6 1.2 fusion.5
  10.8 7.1 %gather_fusion = bf16[1536,2048]{1,0:T(8,128)(2,1)} fusion(bf16[96,2048]{1,0:T(8,128)(2,1)S(1)} %fusion.5, s32[2048]{0:T(1024)S(1)} %pad_clamp_fusion), kind=kCustom, calls=%fused_computation | custom fusion | bytes 12589056 | tf_op jit(solution)/shard_map/jit(_take)/gather | solution.py:45
  17.9 3.3 %broadcast_select_fusion = bf16[64,24,2048]{2,1,0:T(8,128)(2,1)S(1)} fusion(bf16[64,24,2048]{2,1,0:T(8,128)(2,1)} %bitcast.49, pred[64,24]{1,0:T(8,128)(4,1)S(1)} %broadcast_in_dim.41), kind=kLoop, calls=%fused_computation.6 | loop fusion | flops 3145728 | bytes 12584448 | tf_op jit(solution)/shard_map/jit(_take)/select_n | solution.py:45
  21.1 76.9 %all_to_all.33 = bf16[64,24,2048]{2,1,0:T(8,128)(2,1)S(1)} all-to-all(bf16[64,24,2048]{2,1,0:T(8,128)(2,1)S(1)} %broadcast_select_fusion), channel_id=1, replica_groups=mesh['dp'=2,'ep'=8] {'ep'}, dimensions={0} | all-to-all | bytes 12582912 | tf_op jit(solution)/shard_map/all_to_all | solution.py:46
  98.1 3.2 %copy.40 = bf16[8,8,24,2048]{3,2,1,0:T(8,128)(2,1)} copy(bf16[8,8,24,2048]{3,2,0,1:T(8,128)(2,1)S(1)} %bitcast.46) | data formatting | bytes 12582912 | tf_op jit(solution)/shard_map/all_to_all | solution.py:46
  101.3 18.3 %fusion.22 = f32[8,192,1024]{2,1,0:T(8,128)} fusion(bf16[8,192,2048]{2,1,0:T(8,128)(2,1)} %bitcast.47, bf16[8,2048,1024]{2,1,0:T(8,128)(2,1)} %param.11), kind=kOutput, calls=%fused_computation.56 | convolution fusion | flops 6442450944 | bytes 46137344 | tf_op jit(solution)/shard_map/erd,edf->erf/dot_general | solution.py:29
  119.6 30.3 %convolution_convert_fusion = bf16[8,192,2048]{2,1,0:T(8,128)(2,1)} fusion(bf16[8,1024,2048]{2,1,0:T(8,128)(2,1)} %param.13, f32[8,192,1024]{2,1,0:T(8,128)} %fusion.22, bf16[8,192,2048]{2,1,0:T(8,128)(2,1)} %bitcast.48, bf16[8,2048,1024]{2,1,0:T(8,128)(2,1)} %param.12), kind=kOutput, calls=%fused_computation.7 | convolution fusion | flops 12897484800 | bytes 85983232 | tf_op jit(solution)/shard_map/erf,efd->erd/dot_general | solution.py:32
  150.0 8.9 %copy.41 = bf16[8,192,2048]{2,0,1:T(8,128)(2,1)} copy(bf16[8,192,2048]{2,1,0:T(8,128)(2,1)} %convolution_convert_fusion) | data formatting | bytes 12582912 | tf_op jit(solution)/shard_map/convert_element_type | solution.py:32
  158.8 0.0 copy-start.1
  158.9 5.8 %all-to-all-start.1 = ((bf16[8,192,2048]{2,0,1:T(8,128)(2,1)}), bf16[8,192,2048]{2,0,1:T(8,128)(2,1)}, u32[]{:S(2)}, u32[]{:S(2)}) async-start(bf16[8,192,2048]{2,0,1:T(8,128)(2,1)} %copy.41), calls=%async_computation.1 | async-start | bytes 12582912 | tf_op jit(solution)/shard_map/all_to_all | solution.py:48
  164.7 0.1 reduce_sum.50
  164.8 0.0 copy-done.1
  164.8 0.1 copy.43
  164.9 0.1 reshape.129
  165.0 0.1 copy.37
  165.1 0.1 copy.38
  165.2 0.0 copy-done
  165.2 0.3 fusion.21
  165.5 5.1 %gather_fusion.2 = f32[768]{0:T(1024)S(1)} fusion(f32[96,64]{0,1:T(8,128)S(1)} %fusion.11, s32[768]{0:T(1024)S(1)} %reshape.129), kind=kCustom, calls=%fused_computation.2 | custom fusion | bytes 12288 | tf_op jit(solution)/shard_map/jit(take_along_axis)/gather | solution.py:15
  170.7 0.1 reshape.132
  170.8 0.1 copy.44
  170.9 0.1 copy.45
  171.0 64.9 %all-to-all-done.1 = bf16[8,192,2048]{2,0,1:T(8,128)(2,1)} async-done(((bf16[8,192,2048]{2,0,1:T(8,128)(2,1)}), bf16[8,192,2048]{2,0,1:T(8,128)(2,1)}, u32[]{:S(2)}, u32[]{:S(2)}) %all-to-all-start.1) | async-done | bytes 6291488 | tf_op jit(solution)/shard_map/all_to_all | solution.py:48
  235.8 9.5 %copy.42 = bf16[8,8,24,2048]{3,2,0,1:T(8,128)(2,1)} copy(bf16[8,8,24,2048]{3,0,2,1:T(8,128)(2,1)} %bitcast.5) | data formatting | bytes 12582912 | tf_op jit(solution)/shard_map/all_to_all | solution.py:48
  245.3 9.9 %gather_fusion.1 = bf16[768,2048]{1,0:T(8,128)(2,1)S(1)} fusion(bf16[1536,2048]{1,0:T(8,128)(2,1)} %bitcast.45, s32[1024]{0:T(1024)S(1)} %pad_clamp_fusion.1), kind=kCustom, calls=%fused_computation.1 | custom fusion | bytes 6294528 | tf_op jit(solution)/shard_map/jit(_take)/gather | solution.py:49
  255.3 2.7 %multiply_reduce_fusion = f32[96,2048]{1,0:T(8,128)S(1)} fusion(bf16[768,2048]{1,0:T(8,128)(2,1)S(1)} %gather_fusion.1, f32[96,8]{1,0:T(8,128)S(1)} %copy.45, pred[96,8]{1,0:T(8,128)(4,1)S(1)} %copy.38), kind=kLoop, calls=%fused_computation.4 | loop fusion | flops 6094848 | bytes 3936000 | tf_op jit(solution)/shard_map/reduce_sum | solution.py:50
  258.0 1.8 fusion.6
  (15 shorter events, 0.2 us)
Async XLA Ops:
  0.0 165.2 %copy-start = (bf16[2048,64]{0,1:T(8,128)(2,1)S(1)}, bf16[2048,64]{0,1:T(8,128)(2,1)}, u32[]{:S(2)}) copy-start(bf16[2048,64]{0,1:T(8,128)(2,1)} %param.9) | copy-start | bytes 786436
  158.8 5.9 %copy-start.1 = (s32[96,8]{0,1:T(8,128)S(1)}, s32[96,8]{0,1:T(8,128)}, u32[]{:S(2)}) copy-start(s32[96,8]{0,1:T(8,128)} %param.10) | copy-start | bytes 9220
  158.9 77.0 %all-to-all-start.1 = ((bf16[8,192,2048]{2,0,1:T(8,128)(2,1)}), bf16[8,192,2048]{2,0,1:T(8,128)(2,1)}, u32[]{:S(2)}, u32[]{:S(2)}) async-start(bf16[8,192,2048]{2,0,1:T(8,128)(2,1)} %copy.41), calls=%async_computation.1 | async-start | bytes 12582912 | tf_op jit(solution)/shard_map/all_to_all | solution.py:48
where the time goes:
time: 261 us; the launch traced here: 260 us
  blocking collectives  76.9 us (29%)
  waiting for transfers between devices  64.9 us (25%)
  local copies, waits for them, and re-layouts  49.3 us (19%)
  matrix products  48.9 us (19%)
  other arithmetic  13.8 us (5%)
  starting transfers between devices  5.85 us (2%)
    all_to_all x1, blocking collectives, local_block(): received = lax.all_to_all(outgoing, 'ep', 0, 1, tiled=True)  76.9 us
    all_to_all x1, waiting for transfers between devices, local_block(): lax.all_to_all(outputs, 'ep', 1, 0, tiled=True)  64.9 us
    dot_general x1, matrix products, expert_mlp(): jnp.einsum('erf,efd->erd', hidden_act, w_down, preferred_element_type=jnp...  30.3 us
    dot_general x1, matrix products, expert_mlp(): jnp.einsum('erd,edf->erf', rows, w_gate, preferred_element_type=jnp.float32)  18.3 us
    gather x1, local copies, waits for them, and re-layouts, local_block(): y_sel = jnp.take(returned, slots, axis=0).reshape(tokens, top_k, hidden)  9.93 us
    all_to_all x1, local copies, waits for them, and re-layouts, local_block(): lax.all_to_all(outputs, 'ep', 1, 0, tiled=True)  9.51 us
    convert_element_type x1, local copies, waits for them, and re-layouts, expert_mlp(): jnp.einsum('erf,efd->erd', hidden_act, w_down, preferred_element_type=jnp...  8.88 us
    gather x1, local copies, waits for them, and re-layouts, local_block(): jnp.take(normed, slot_tok, axis=0, mode='fill', fill_value=0)  7.09 us
  transfers between devices with their start and end apart: 1, of which 1 were waited for; matrix products, arithmetic and copies ran while one was open for 2% of the time, Pallas kernels for 0%

commit v1 on v0

v1 whole, which is shorter than its diff:
```python
import functools

import jax
import jax.numpy as jnp
from jax import lax
from jax.experimental import pallas as pl
from jax.experimental.pallas import tpu as pltpu
from jax.sharding import PartitionSpec as P

EPS = 1e-6
F32 = jnp.float32
BF16 = jnp.bfloat16
COLS = 256
LANES = 128
RING = 8


def dot(a, b):
    return jnp.dot(a, b, preferred_element_type=F32)


def moe_kernel(
    x_ref, gain_ref, wr_ref, ids_ref, wg_ref, wu_ref, wd_ref, out_ref,
    wbuf, xbuf, hbuf, xe, act, oh, gates, a3, ybuf, ps, d2d, far, fin, lg, ids_all, soft, mask,
    wsem, ids_s, ids_r, ag_s, ag_r, d2d_s, d2d_r, far_s, far_r, fin_s, fin_r,
):
    tokens, hidden = x_ref.shape
    local_experts = act.shape[0]
    experts = wr_ref.shape[1]
    chips = xbuf.shape[0]
    half = tokens // 2
    pair_cap = oh.shape[0] // local_experts
    cap = pair_cap // 2
    chunks = hidden // COLS

    me = lax.axis_index("ep")
    chip, core = me // 2, lax.rem(me, 2)

    def device(r, q):
        return {"ep": lax.rem(chip + r, chips) * 2 + (lax.rem(core + q, 2))}

    right, left, peer = device(1, 0), device(chips - 1, 0), device(0, 1)

    def remote(src, dst, send, recv, to):
        return pltpu.make_async_remote_copy(
            src_ref=src, dst_ref=dst, send_sem=send, recv_sem=recv,
            device_id=to, device_id_type=pl.DeviceIdType.MESH,
        )

    def start_gate_up(e):
        slot = 2 * lax.rem(e, RING // 2)
        for k, w in enumerate((wg_ref, wu_ref)):
            for n in range(4):
                pltpu.make_async_copy(
                    w.at[e, :, :, pl.ds(n * COLS, COLS)], wbuf.at[slot + k, pl.ds(2 * n, 2)], wsem.at[slot + k]
                ).start()

    def start_down(n):
        for m in range(4):
            pltpu.make_async_copy(
                wd_ref.at[pl.ds(2 * m, 2), :, pl.ds(pl.multiple_of(n * COLS, COLS), COLS)],
                wbuf.at[n, pl.ds(2 * m, 2)], wsem.at[n]
            ).start()

    def wait_slot(slot):
        pltpu.make_async_copy(wbuf.at[slot], wbuf.at[slot], wsem.at[slot]).wait()

    for e in range(RING // 2):
        start_gate_up(e)

    soft[...] = jnp.full(soft.shape, -1.0, F32)
    soft[pl.ds(0, tokens), pl.ds(0, ids_ref.shape[1])] = ids_ref[...].astype(F32)
    ids_all[0, 0] = soft[:, 0:LANES].T[0:8, :]

    barrier = pltpu.get_barrier_semaphore()
    others = [(r, q) for r in range(chips) for q in range(2) if (r, q) != (0, 0)]
    for r, q in others:
        pl.semaphore_signal(barrier, inc=1, device_id=device(r, q), device_id_type=pl.DeviceIdType.MESH)
    pl.semaphore_wait(barrier, len(others))

    top, bot = pl.ds(0, half), pl.ds(half, half)
    last = chips - 1
    c_r0 = remote(x_ref.at[top], xbuf.at[last, 0, top], ag_s.at[0], ag_r.at[last, 0, 0], right)
    c_l1 = remote(x_ref.at[bot], xbuf.at[1, 0, bot], ag_s.at[1], ag_r.at[1, 0, 1], left)
    c_r1 = remote(x_ref.at[bot], xbuf.at[last, 0, bot], ag_s.at[2], ag_r.at[last, 0, 1], right)
    c_l0 = remote(x_ref.at[top], xbuf.at[1, 0, top], ag_s.at[3], ag_r.at[1, 0, 0], left)
    c_p = remote(x_ref, xbuf.at[0, 1], ag_s.at[4], ag_r.at[0, 1, 0], peer)
    ids_c = {}
    for r, q in others:
        back = (chips - r) % chips
        ids_c[(back, q)] = remote(
            ids_all.at[0, 0], ids_all.at[back, q], ids_s.at[r, q], ids_r.at[back, q], device(r, q)
        )
    ids_c[(0, 1)].start()
    c_p.start()
    for k in others:
        if k != (0, 1):
            ids_c[k].start()
    for c in (c_r0, c_l1, c_r1, c_l0):
        c.start()
    f_r = remote(xbuf.at[last, 0, top], xbuf.at[2, 0, top], ag_s.at[5], ag_r.at[2, 0, 0], right)
    f_l = remote(xbuf.at[1, 0, bot], xbuf.at[2, 0, bot], ag_s.at[6], ag_r.at[2, 0, 1], left)
    cross = {}
    for k, r in enumerate((last, 1, 2)):
        for h, rows in enumerate((top, bot)):
            cross[(r, h)] = remote(
                xbuf.at[r, 0, rows], xbuf.at[r, 1, rows], ag_s.at[7 + 2 * k + h], ag_r.at[r, 1, h], peer
            )

    hbuf[...] = jnp.zeros_like(hbuf)
    gain = gain_ref[...].astype(F32)
    tri = (
        lax.broadcasted_iota(jnp.int32, (LANES, LANES), 0) < lax.broadcasted_iota(jnp.int32, (LANES, LANES), 1)
    ).astype(BF16)

    def process(r, sources):
        for q, src in enumerate(sources):
            def norm_rows(g, carry, q=q, src=src):
                rows = pl.ds(pl.multiple_of(g * 16, 16), 16)
                v = src[rows, :].astype(F32)
                ms = jnp.mean(v * v, axis=-1, keepdims=True)
                hv = (v * lax.rsqrt(ms + EPS) * gain).astype(BF16)
                hbuf[pl.ds(pl.multiple_of(q * LANES + g * 16, 16), 16), :] = hv
                return carry
            lax.fori_loop(0, tokens // 16, norm_rows, 0)
        lg[:, 0:experts] = dot(hbuf[...], wr_ref[...])
        logits = lg[...].T[0:experts, :]
        shifted = jnp.exp(logits - jnp.max(logits, axis=0, keepdims=True))
        prob = shifted / jnp.sum(shifted, axis=0, keepdims=True)
        ids = jnp.concatenate([ids_all[r, 0], ids_all[r, 1]], axis=1)
        eid = lax.broadcasted_iota(jnp.int32, prob.shape, 0).astype(F32)
        chosen = eid == ids[0:1, :]
        for j in range(1, ids.shape[0]):
            chosen = chosen | (eid == ids[j : j + 1, :])
        picked = jnp.where(chosen, prob, 0.0)
        gate_all = jnp.where(chosen, picked / jnp.sum(picked, axis=0, keepdims=True), 0.0)
        soft[0:experts, :] = gate_all
        mask[...] = jnp.where(chosen, 1.0, 0.0)
        mine = pl.ds(pl.multiple_of(me * local_experts, local_experts), local_experts)
        gate = soft[mine, :]
        hit = mask[mine, :]
        pos = jnp.concatenate(
            [dot(hit[:, q * LANES : (q + 1) * LANES].astype(BF16), tri) + float(q * cap) for q in range(2)], axis=1
        )
        pos = jnp.where(hit > 0.5, pos, -1.0)
        slot = lax.broadcasted_iota(jnp.int32, (pair_cap, 2 * LANES), 0).astype(F32)
        for e in range(local_experts):
            here = slot == pos[e : e + 1, :]
            oh[pl.ds(e * pair_cap, pair_cap), :] = jnp.where(here, 1.0, 0.0).astype(BF16)
            gates[pl.ds(e * pair_cap, pair_cap), :] = jnp.where(here, gate[e : e + 1, :], 0.0)

        def gather_cols(n, carry):
            cols = pl.ds(pl.multiple_of(n * COLS, COLS), COLS)
            res = dot(oh[...], hbuf[:, cols]).astype(BF16)
            for e in range(local_experts):
                xe[e, pl.ds(r * pair_cap, pair_cap), cols] = res[e * pair_cap : (e + 1) * pair_cap]
            return carry
        lax.fori_loop(0, hidden // COLS, gather_cols, 0)

        gt = gates[...].T
        hi = gt.astype(BF16)
        rest = gt - hi.astype(F32)
        mid = rest.astype(BF16)
        low = (rest - mid.astype(F32)).astype(BF16)
        for k, part in enumerate((hi, mid, low)):
            for q in range(2):
                a3[r, pl.ds((2 * k + q) * tokens, tokens), :] = part[q * LANES : q * LANES + tokens]

    def ids_wait(r):
        for q in range(2):
            if (r, q) != (0, 0):
                ids_c[(r, q)].wait_recv()

    ids_wait(0)
    c_p.wait_recv()
    process(0, (x_ref, xbuf.at[0, 1]))
    c_r0.wait_recv()
    f_r.start()
    cross[(last, 0)].start()
    c_l1.wait_recv()
    f_l.start()
    cross[(1, 1)].start()
    c_r1.wait_recv()
    cross[(last, 1)].start()
    c_l0.wait_recv()
    cross[(1, 0)].start()
    for r in (last, 1):
        ids_wait(r)
        cross[(r, 0)].wait_recv()
        cross[(r, 1)].wait_recv()
        process(r, (xbuf.at[r, 0], xbuf.at[r, 1]))
    f_r.wait_recv()
    cross[(2, 0)].start()
    f_l.wait_recv()
    cross[(2, 1)].start()
    ids_wait(2)
    cross[(2, 0)].wait_recv()
    cross[(2, 1)].wait_recv()
    process(2, (xbuf.at[2, 0], xbuf.at[2, 1]))

    def expert(e, carry):
        slot = 2 * lax.rem(e, RING // 2)
        wait_slot(slot)
        wait_slot(slot + 1)
        rows = xe[e]
        for n in range(4):
            g = dot(rows, wbuf[slot, 2 * n : 2 * n + 2].reshape(hidden, COLS))
            u = dot(rows, wbuf[slot + 1, 2 * n : 2 * n + 2].reshape(hidden, COLS))
            act[e, :, n * COLS : (n + 1) * COLS] = (g * jax.nn.sigmoid(g) * u).astype(BF16)

        @pl.when(e < local_experts - RING // 2)
        def _():
            start_gate_up(e + RING // 2)

        @pl.when(e >= local_experts - RING // 2)
        def _():
            n = 2 * (e - (local_experts - RING // 2))
            start_down(n)
            start_down(n + 1)
        return carry

    lax.fori_loop(0, local_experts, expert, 0)

    def cross_copy(n):
        return remote(ps.at[n, 1], d2d.at[n], d2d_s.at[n], d2d_r.at[n], peer)

    def far_copies(n):
        return (
            remote(ps.at[n, 0, 2, 0], far.at[n, 0], far_s.at[n, 0], far_r.at[n, 0], right),
            remote(ps.at[n, 0, 2, 1], far.at[n, 1], far_s.at[n, 1], far_r.at[n, 1], left),
        )

    def near_copies(n):
        return (
            remote(ps.at[n, 0, 1, 1], fin.at[n, 0, 1], fin_s.at[n, 0, 1], fin_r.at[n, 0, 1], right),
            remote(ps.at[n, 0, last, 0], fin.at[n, 1, 0], fin_s.at[n, 1, 0], fin_r.at[n, 1, 0], left),
        )

    def sum_copies(n):
        return (
            remote(ps.at[n, 0, 1, 0], fin.at[n, 0, 0], fin_s.at[n, 0, 0], fin_r.at[n, 0, 0], right),
            remote(ps.at[n, 0, last, 1], fin.at[n, 1, 1], fin_s.at[n, 1, 1], fin_r.at[n, 1, 1], left),
        )

    def stage1(n):
        cross_copy(n).wait_recv()
        for r in (2, 1, last, 0):
            ps[n, 0, r] = ps[n, 0, r] + d2d[n, r]
        for c in far_copies(n) + near_copies(n):
            c.start()

    def chunk(n, carry):
        wait_slot(n)
        for e in range(local_experts):
            y = dot(act[e], wbuf[n, e]).astype(BF16)
            for r in range(chips):
                ybuf[r, pl.ds(e * pair_cap, pair_cap), :] = y[r * pair_cap : (r + 1) * pair_cap]
        for r in range(chips):
            parts = dot(a3[r], ybuf[r])
            t = 2 * tokens
            total = parts[0:t] + (parts[t : 2 * t] + parts[2 * t : 3 * t])
            for q in range(2):
                for h in range(2):
                    ps[n, q, r, h] = total[q * tokens : (q + 1) * tokens, h * LANES : (h + 1) * LANES]
        cross_copy(n).start()

        @pl.when(n > 0)
        def _():
            stage1(n - 1)
        return carry

    lax.fori_loop(0, chunks, chunk, 0)
    stage1(chunks - 1)

    def stage2(n, carry):
        from_left, from_right = far_copies(n)
        to_right, to_left = sum_copies(n)
        from_left.wait_recv()
        ps[n, 0, 1, 0] = ps[n, 0, 1, 0] + far[n, 0]
        to_right.start()
        from_right.wait_recv()
        ps[n, 0, last, 1] = ps[n, 0, last, 1] + far[n, 1]
        to_left.start()
        return carry

    lax.fori_loop(0, chunks, stage2, 0)

    def final(n, carry):
        for c in near_copies(n) + sum_copies(n):
            c.wait_recv()
        for h in range(2):
            cols = pl.ds(pl.multiple_of(n * COLS + h * LANES, LANES), LANES)
            total = ps[n, 0, 0, h] + fin[n, 0, h] + fin[n, 1, h]
            out_ref[:, cols] = (x_ref[:, cols].astype(F32) + total).astype(BF16)
        return carry

    lax.fori_loop(0, chunks, final, 0)

    def drain(n, carry):
        cross_copy(n).wait_send()
        for c in far_copies(n) + near_copies(n) + sum_copies(n):
            c.wait_send()
        return carry

    lax.fori_loop(0, chunks, drain, 0)
    for c in [c_r0, c_l1, c_r1, c_l0, c_p, f_r, f_l] + list(ids_c.values()) + list(cross.values()):
        c.wait_send()


def solution(mesh):
    group = mesh.shape["ep"]
    chips = group // 2

    def local_block(x_in, norm_gain, w_router, expert_ids, w_gate, w_up, w_down):
        tokens, hidden = x_in.shape
        experts = w_router.shape[1]
        top_k = expert_ids.shape[1]
        local_experts, _, ff = w_gate.shape
        cap = 2 * tokens * top_k // experts
        rows = local_experts * 2 * cap
        chunks = hidden // COLS
        wg = w_gate.reshape(local_experts, 2, hidden // 2, ff)
        wu = w_up.reshape(local_experts, 2, hidden // 2, ff)
        vmem = pl.BlockSpec(memory_space=pltpu.VMEM)
        hbm = pl.BlockSpec(memory_space=pl.ANY)
        dma = pltpu.SemaphoreType.DMA
        return pl.pallas_call(
            moe_kernel,
            out_shape=jax.ShapeDtypeStruct((tokens, hidden), BF16),
            in_specs=[vmem, vmem, vmem, vmem, hbm, hbm, hbm],
            out_specs=vmem,
            scratch_shapes=[
                pltpu.VMEM((RING, local_experts, ff, COLS), BF16),
                pltpu.VMEM((chips, 2, tokens, hidden), BF16),
                pltpu.VMEM((2 * LANES, hidden), BF16),
                pltpu.VMEM((local_experts, group * cap, hidden), BF16),
                pltpu.VMEM((local_experts, group * cap, ff), BF16),
                pltpu.VMEM((rows, 2 * LANES), BF16),
                pltpu.VMEM((rows, 2 * LANES), F32),
                pltpu.VMEM((chips, 6 * tokens, rows), BF16),
                pltpu.VMEM((chips, rows, COLS), BF16),
                pltpu.VMEM((chunks, 2, chips, 2, tokens, LANES), F32),
                pltpu.VMEM((chunks, chips, 2, tokens, LANES), F32),
                pltpu.VMEM((chunks, 2, tokens, LANES), F32),
                pltpu.VMEM((chunks, 2, 2, tokens, LANES), F32),
                pltpu.VMEM((2 * LANES, LANES), F32),
                pltpu.VMEM((chips, 2, 8, LANES), F32),
                pltpu.VMEM((LANES, 2 * LANES), F32),
                pltpu.VMEM((experts, 2 * LANES), F32),
                dma((RING,)),
                dma((chips, 2)), dma((chips, 2)),
                dma((13,)), dma((chips, 2, 2)),
                dma((chunks,)), dma((chunks,)),
                dma((chunks, 2)), dma((chunks, 2)),
                dma((chunks, 2, 2)), dma((chunks, 2, 2)),
            ],
            compiler_params=pltpu.CompilerParams(
                collective_id=0, has_side_effects=True, vmem_limit_bytes=67043328
            ),
        )(x_in, norm_gain.reshape(1, hidden), w_router, expert_ids, wg, wu, w_down)

    tok_spec = P(("dp", "ep"), None)
    expert_spec = P("ep", None, None)
    return jax.shard_map(local_block, mesh=mesh, in_specs=(tok_spec, P(None), P(None, None), tok_spec, expert_spec, expert_spec, expert_spec), out_specs=tok_spec, check_vma=False)
```

time: 261 us -> 85.4 us (0.33)
  Pallas kernels: 0 us -> 78.7 us
  blocking collectives: 76.9 us -> 0 us
  waiting for transfers between devices: 64.9 us -> 0 us
  matrix products: 48.9 us -> 0 us
  local copies, waits for them, and re-layouts: 49.3 us -> 6.39 us
  other arithmetic: 13.8 us -> 0 us
  starting transfers between devices: 5.85 us -> 0 us
    pallas_call x0 -> x1, Pallas kernels: none -> 78.7 us  [local_block(): pl.pallas_call(moe_kernel, out_shape=jax.ShapeDtypeStruct((tokens, hidden...]
    all_to_all x1 -> x0, blocking collectives: 76.9 us -> none  [local_block(): received = lax.all_to_all(outgoing, 'ep', 0, 1, tiled=True)]
    all_to_all x1 -> x0, waiting for transfers between devices: 64.9 us -> none  [local_block(): lax.all_to_all(outputs, 'ep', 1, 0, tiled=True)]
    dot_general x3 -> x0, matrix products: 48.9 us -> none  [the longest x1 30.3 us: expert_mlp(): jnp.einsum('erf,efd->erd', hidden_act, w_down, preferred_element_type=jnp...]
    gather x7 -> x0, local copies, waits for them, and re-layouts: 22.5 us -> none  [the longest x1 9.93 us: local_block(): y_sel = jnp.take(returned, slots, axis=0).reshape(tokens, top_k, hidden)]
    all_to_all x2 -> x0, local copies, waits for them, and re-layouts: 12.7 us -> none  [the longest x1 9.51 us: local_block(): lax.all_to_all(outputs, 'ep', 1, 0, tiled=True)]
    convert_element_type x1 -> x0, local copies, waits for them, and re-layouts: 8.88 us -> none  [expert_mlp(): jnp.einsum('erf,efd->erd', hidden_act, w_down, preferred_element_type=jnp...]
    all_to_all x1 -> x0, starting transfers between devices: 5.85 us -> none  [local_block(): lax.all_to_all(outputs, 'ep', 1, 0, tiled=True)]
  transfers between devices with their start and end apart: 1 -> 0, of which waited for: 1 -> 0; matrix products, arithmetic and copies ran while one was open for 2% -> 0% of each run, Pallas kernels for 0% -> 0%
where the time goes in v1:
time: 85.4 us; the launch traced here: 85.1 us
  Pallas kernels  78.7 us (92%)
  local copies, waits for them, and re-layouts  6.39 us (7%)
    pallas_call x1, Pallas kernels, local_block(): pl.pallas_call(moe_kernel, out_shape=jax.ShapeDtypeStruct((tokens, hidden...  78.7 us
    unnamed x3, local copies, waits for them, and re-layouts  5.11 us

profile of v1, /device:TPU:113, one launch (start us, length us, event | category | flops | bytes accessed | tf_op | source)
XLA Modules:
  0.0 85.1 jit_solution(15287715995313275986)
XLA Ops:
  0.0 1.3 %reshape.9.gain_ref = bf16[1,2048]{1,0:T(2,128)(2,1)} reshape(bf16[2048]{0:T(1024)(128)(2,1)} %param.8) | data formatting | bytes 8192 | tf_op jit(solution)/shard_map/reshape | solution.py:360
  1.3 1.4 %copy.9.ids_ref = s32[96,8]{1,0:T(8,128)} copy(s32[96,8]{0,1:T(8,128)} %param.10) | data formatting | bytes 6144 | tf_op args[3]
  2.7 1.9 %copy.8.wr_ref = bf16[2048,64]{1,0:T(8,128)(2,1)} copy(bf16[2048,64]{0,1:T(8,128)(2,1)} %param.9) | data formatting | bytes 524288 | tf_op args[2]
  4.6 78.7 %shard_map.73 = bf16[96,2048]{1,0:T(8,128)(2,1)} custom-call(bf16[96,2048]{1,0:T(8,128)(2,1)} %x_ref.1, bf16[1,2048]{1,0:T(2,128)(2,1)} %reshape.9.gain_ref, bf16[2048,64]{1,0:T(8,128)(2,1)} %copy.8.wr_ref, s32[96,8]{1,0:T(8,128)} %copy.9.ids_ref, bf16[8,2,1024,1024]{3,2,1,0:T(8,128)(2,1)} %bitcast.2, bf16[8,2,1024,1024]{3,2,1,0:T(8,128)(2,1)} %bitcast.3, ...), custom_call_target="tpu_custom_call" | custom-call | tf_op jit(solution)/shard_map/pallas_call | solution.py:327
  83.3 1.8 %copy.11 = bf16[96,2048]{1,0:T(8,128)(2,1)} copy(bf16[96,2048]{1,0:T(8,128)(2,1)} %shard_map.73) | data formatting | bytes 786432

commit v2 on v1

v2 whole, which is shorter than its diff:
```python
import functools

import jax
import jax.numpy as jnp
from jax import lax
from jax.experimental import pallas as pl
from jax.experimental.pallas import tpu as pltpu
from jax.sharding import PartitionSpec as P

EPS = 1e-6
F32 = jnp.float32
BF16 = jnp.bfloat16
COLS = 256
LANES = 128
RING = 8


def dot(a, b):
    return jnp.dot(a, b, preferred_element_type=F32)


def moe_kernel(
    x_hbm, gain_hbm, wr_hbm, ids_hbm, wg_ref, wu_ref, wd_ref, out_ref,
    x_ref, gain_ref, wr_ref, ids_ref,
    wbuf, xbuf, hbuf, xe, act, oh, gates, a3, ybuf, ps, d2d, far, fin, ids_all, soft, mask,
    in_sem, wsem, ids_s, ids_r, ag_s, ag_r, d2d_s, d2d_r, far_s, far_r, fin_s, fin_r,
):
    tokens, hidden = x_ref.shape
    local_experts = act.shape[0]
    experts = wr_ref.shape[0]
    chips = xbuf.shape[0]
    half = tokens // 2
    pair_cap = oh.shape[0] // local_experts
    own_cap = 2 * pair_cap // 3
    chunks = hidden // COLS

    me = lax.axis_index("ep")
    chip, core = me // 2, lax.rem(me, 2)

    def device(r, q):
        return {"ep": lax.rem(chip + r, chips) * 2 + (lax.rem(core + q, 2))}

    right, left, peer = device(1, 0), device(chips - 1, 0), device(0, 1)

    def remote(src, dst, send, recv, to):
        return pltpu.make_async_remote_copy(
            src_ref=src, dst_ref=dst, send_sem=send, recv_sem=recv,
            device_id=to, device_id_type=pl.DeviceIdType.MESH,
        )

    def start_gate_up(e):
        slot = 2 * lax.rem(e, RING // 2)
        for k, w in enumerate((wg_ref, wu_ref)):
            for n in range(4):
                pltpu.make_async_copy(
                    w.at[e, :, :, pl.ds(n * COLS, COLS)], wbuf.at[slot + k, pl.ds(2 * n, 2)], wsem.at[slot + k]
                ).start()

    def start_down(n):
        for m in range(4):
            pltpu.make_async_copy(
                wd_ref.at[pl.ds(2 * m, 2), :, pl.ds(pl.multiple_of(n * COLS, COLS), COLS)],
                wbuf.at[n, pl.ds(2 * m, 2)], wsem.at[n]
            ).start()

    def wait_slot(slot):
        pltpu.make_async_copy(wbuf.at[slot], wbuf.at[slot], wsem.at[slot]).wait()

    barrier = pltpu.get_barrier_semaphore()
    others = [(r, q) for r in range(chips) for q in range(2) if (r, q) != (0, 0)]
    for r, q in others:
        pl.semaphore_signal(barrier, inc=1, device_id=device(r, q), device_id_type=pl.DeviceIdType.MESH)
    inputs = [
        pltpu.make_async_copy(a, b, in_sem.at[k])
        for k, (a, b) in enumerate(((ids_hbm, ids_ref), (x_hbm, x_ref), (gain_hbm, gain_ref), (wr_hbm, wr_ref)))
    ]
    for c in inputs:
        c.start()

    ids_all[0, 0] = jnp.full(ids_all.shape[2:], -1.0, F32)
    with jax.named_scope("inputs"):
        for c in inputs:
            c.wait()
    ids_all[0, 0, :, 0:tokens] = ids_ref[...].astype(F32)
    for e in range(RING // 2):
        start_gate_up(e)
    with jax.named_scope("barrier"):
        pl.semaphore_wait(barrier, len(others))

    top, bot = pl.ds(0, half), pl.ds(half, half)
    last = chips - 1
    c_r0 = remote(x_ref.at[top], xbuf.at[last, 0, top], ag_s.at[0], ag_r.at[last, 0, 0], right)
    c_l1 = remote(x_ref.at[bot], xbuf.at[1, 0, bot], ag_s.at[1], ag_r.at[1, 0, 1], left)
    c_r1 = remote(x_ref.at[bot], xbuf.at[last, 0, bot], ag_s.at[2], ag_r.at[last, 0, 1], right)
    c_l0 = remote(x_ref.at[top], xbuf.at[1, 0, top], ag_s.at[3], ag_r.at[1, 0, 0], left)
    c_p = remote(x_ref, xbuf.at[0, 1], ag_s.at[4], ag_r.at[0, 1, 0], peer)
    ids_c = {}
    for r, q in others:
        back = (chips - r) % chips
        ids_c[(back, q)] = remote(
            ids_all.at[0, 0], ids_all.at[back, q], ids_s.at[r, q], ids_r.at[back, q], device(r, q)
        )
    ids_c[(0, 1)].start()
    c_p.start()
    for k in others:
        if k != (0, 1):
            ids_c[k].start()
    for c in (c_r0, c_l1, c_r1, c_l0):
        c.start()
    f_r = remote(xbuf.at[last, 0, top], xbuf.at[2, 0, top], ag_s.at[5], ag_r.at[2, 0, 0], right)
    f_l = remote(xbuf.at[1, 0, bot], xbuf.at[2, 0, bot], ag_s.at[6], ag_r.at[2, 0, 1], left)
    cross = {}
    for k, r in enumerate((last, 1, 2)):
        for h, rows in enumerate((top, bot)):
            cross[(r, h)] = remote(
                xbuf.at[r, 0, rows], xbuf.at[r, 1, rows], ag_s.at[7 + 2 * k + h], ag_r.at[r, 1, h], peer
            )

    for k in range(hbuf.shape[0]):
        for q in range(2):
            hbuf[k, q * LANES + tokens : (q + 1) * LANES, :] = jnp.zeros((LANES - tokens, hidden), BF16)
    gain = jnp.concatenate([gain_ref[k : k + 1, :] for k in range(gain_ref.shape[0])], axis=1).astype(F32)
    tri = (
        lax.broadcasted_iota(jnp.int32, (LANES, LANES), 0) < lax.broadcasted_iota(jnp.int32, (LANES, LANES), 1)
    ).astype(BF16)

    def norm(src, k, q, h):
        for g in range(half // 16):
            row = h * half + g * 16
            v = src[row : row + 16, :].astype(F32)
            ms = jnp.mean(v * v, axis=-1, keepdims=True)
            hbuf[k, q * LANES + row : q * LANES + row + 16, :] = (v * lax.rsqrt(ms + EPS) * gain).astype(BF16)

    def route(r, k):
        logits = lax.dot_general(
            wr_ref[...], hbuf[k], (((1,), (1,)), ((), ())), preferred_element_type=F32
        )
        shifted = jnp.exp(logits - jnp.max(logits, axis=0, keepdims=True))
        prob = shifted / jnp.sum(shifted, axis=0, keepdims=True)
        ids = jnp.concatenate([ids_all[r, 0], ids_all[r, 1]], axis=1)
        eid = lax.broadcasted_iota(jnp.int32, prob.shape, 0).astype(F32)
        chosen = eid == ids[0:1, :]
        for j in range(1, ids.shape[0]):
            chosen = chosen | (eid == ids[j : j + 1, :])
        picked = jnp.where(chosen, prob, 0.0)
        soft[...] = jnp.where(chosen, picked / jnp.sum(picked, axis=0, keepdims=True), 0.0)
        mask[...] = jnp.where(chosen, 1.0, 0.0)
        mine = pl.ds(pl.multiple_of(me * local_experts, local_experts), local_experts)
        gate = soft[mine, :]
        hit = mask[mine, :]
        rows = []
        for q in range(2):
            lanes = slice(q * LANES, (q + 1) * LANES)
            pos = dot(hit[:, lanes].astype(BF16), tri)
            first = pos < 15.5
            own = jnp.where(hit[:, lanes] > 0.5, jnp.where(first, pos, pos + 8.0 * q), -1.0)
            rows.append(jnp.where(hit[:, lanes] > 0.5, jnp.where(first, pos + 16.0 * q, pos + (16.0 + 8.0 * q)), -1.0))
            slot = lax.broadcasted_iota(jnp.int32, (own_cap, LANES), 0).astype(F32)
            for e in range(local_experts):
                gates[r, q, pl.ds(e * own_cap, own_cap), :] = jnp.where(
                    slot == own[e : e + 1, :], gate[e : e + 1, lanes], 0.0
                )
        pair = jnp.concatenate(rows, axis=1)
        slot = lax.broadcasted_iota(jnp.int32, (pair_cap, 2 * LANES), 0).astype(F32)
        for e in range(local_experts):
            oh[pl.ds(e * pair_cap, pair_cap), :] = jnp.where(slot == pair[e : e + 1, :], 1.0, 0.0).astype(BF16)

    def gather(r, k):
        def gather_cols(n, carry):
            for m in range(4):
                cols = pl.ds(pl.multiple_of(n * (4 * COLS) + m * COLS, COLS), COLS)
                res = dot(oh[...], hbuf[k, :, cols]).astype(BF16)
                for e in range(local_experts):
                    xe[e, pl.ds(r * pair_cap, pair_cap), cols] = res[e * pair_cap : (e + 1) * pair_cap]
            return carry
        lax.fori_loop(0, hidden // (4 * COLS), gather_cols, 0)

    def split_gates(r):
        for q in range(2):
            gt = gates[r, q].T[0:tokens]
            hi = gt.astype(BF16)
            rest = gt - hi.astype(F32)
            mid = rest.astype(BF16)
            low = (rest - mid.astype(F32)).astype(BF16)
            for p, part in enumerate((hi, mid, low)):
                a3[r, q, pl.ds(p * tokens, tokens), :] = part

    def tables(r, k):
        with jax.named_scope(f"route#r={r}"):
            route(r, k)
        with jax.named_scope(f"gather#r={r}"):
            gather(r, k)

    def ids_wait(r):
        for q in range(2):
            if (r, q) != (0, 0):
                ids_c[(r, q)].wait_recv()

    def gate_up_rows(e, rows):
        slot = 2 * lax.rem(e, RING // 2)
        data = xe[e, rows, :]
        for n in range(4):
            g = dot(data, wbuf[slot, 2 * n : 2 * n + 2].reshape(hidden, COLS))
            u = dot(data, wbuf[slot + 1, 2 * n : 2 * n + 2].reshape(hidden, COLS))
            act[e, rows, n * COLS : (n + 1) * COLS] = (g * jax.nn.sigmoid(g) * u).astype(BF16)

    own_rows = pl.ds(0, pair_cap)
    rest_rows = pl.ds(pair_cap, (chips - 1) * pair_cap)
    all_rows = pl.ds(0, chips * pair_cap)

    def own_pass(e, carry):
        with jax.named_scope("own_pass"):
            wait_slot(2 * e)
            wait_slot(2 * e + 1)
            gate_up_rows(e, own_rows)
        return carry

    with jax.named_scope("norm_own"):
        norm(x_ref, 0, 0, 0)
        norm(x_ref, 0, 0, 1)
    with jax.named_scope("own_wait"):
        ids_wait(0)
        c_p.wait_recv()
    with jax.named_scope("norm_peer"):
        norm(xbuf.at[0, 1], 0, 1, 0)
        norm(xbuf.at[0, 1], 0, 1, 1)
    tables(0, 0)
    lax.fori_loop(0, 2, own_pass, 0)
    with jax.named_scope("near_wait"):
        c_r0.wait_recv()
        f_r.start()
        cross[(last, 0)].start()
        c_l1.wait_recv()
        f_l.start()
        cross[(1, 1)].start()
    with jax.named_scope("norm_near"):
        norm(xbuf.at[last, 0], 0, 0, 0)
        norm(xbuf.at[1, 0], 1, 0, 1)
        cross[(last, 0)].wait_recv()
        cross[(1, 1)].wait_recv()
        norm(xbuf.at[last, 1], 0, 1, 0)
        norm(xbuf.at[1, 1], 1, 1, 1)
    lax.fori_loop(2, RING // 2, own_pass, 0)
    with jax.named_scope("near_wait2"):
        c_r1.wait_recv()
        cross[(last, 1)].start()
        c_l0.wait_recv()
        cross[(1, 0)].start()
    with jax.named_scope("norm_near2"):
        norm(xbuf.at[last, 0], 0, 0, 1)
        norm(xbuf.at[1, 0], 1, 0, 0)
        cross[(last, 1)].wait_recv()
        cross[(1, 0)].wait_recv()
        norm(xbuf.at[last, 1], 0, 1, 1)
        norm(xbuf.at[1, 1], 1, 1, 0)
    ids_wait(last)
    ids_wait(1)
    tables(last, 0)
    with jax.named_scope("far_wait"):
        f_r.wait_recv()
        cross[(2, 0)].start()
        f_l.wait_recv()
        cross[(2, 1)].start()
    tables(1, 1)
    with jax.named_scope("norm_far"):
        norm(xbuf.at[2, 0], 0, 0, 0)
        norm(xbuf.at[2, 0], 0, 0, 1)
    with jax.named_scope("far_cross_wait"):
        ids_wait(2)
        cross[(2, 0)].wait_recv()
        cross[(2, 1)].wait_recv()
    with jax.named_scope("norm_far2"):
        norm(xbuf.at[2, 1], 0, 1, 0)
        norm(xbuf.at[2, 1], 0, 1, 1)
    tables(2, 0)

    def refill(e):
        @pl.when(e < local_experts - RING // 2)
        def _():
            start_gate_up(e + RING // 2)

        @pl.when(e >= local_experts - RING // 2)
        def _():
            n = 2 * (e - (local_experts - RING // 2))
            start_down(n)
            start_down(n + 1)

    def expert_rest(e, carry):
        with jax.named_scope("gate_up_rest"):
            gate_up_rows(e, rest_rows)
            split_gates(e)
        refill(e)
        return carry

    def expert_all(e, carry):
        slot = 2 * lax.rem(e, RING // 2)
        with jax.named_scope("gate_up_wait"):
            wait_slot(slot)
            wait_slot(slot + 1)
        with jax.named_scope("gate_up"):
            gate_up_rows(e, all_rows)
        refill(e)
        return carry

    lax.fori_loop(0, RING // 2, expert_rest, 0)
    lax.fori_loop(RING // 2, local_experts, expert_all, 0)

    def cross_copy(n, r):
        return remote(ps.at[n, 1, r], d2d.at[n, r], d2d_s.at[n, r], d2d_r.at[n, r], peer)

    def far_copies(n):
        return (
            remote(ps.at[n, 0, 2, 0], far.at[n, 0], far_s.at[n, 0], far_r.at[n, 0], right),
            remote(ps.at[n, 0, 2, 1], far.at[n, 1], far_s.at[n, 1], far_r.at[n, 1], left),
        )

    def near_copies(n):
        return (
            remote(ps.at[n, 0, 1, 1], fin.at[n, 0, 1], fin_s.at[n, 0, 1], fin_r.at[n, 0, 1], right),
            remote(ps.at[n, 0, last, 0], fin.at[n, 1, 0], fin_s.at[n, 1, 0], fin_r.at[n, 1, 0], left),
        )

    def sum_copies(n):
        return (
            remote(ps.at[n, 0, 1, 0], fin.at[n, 0, 0], fin_s.at[n, 0, 0], fin_r.at[n, 0, 0], right),
            remote(ps.at[n, 0, last, 1], fin.at[n, 1, 1], fin_s.at[n, 1, 1], fin_r.at[n, 1, 1], left),
        )

    far_first = (2, 1, last, 0)

    def stage1(n):
        for r in far_first:
            with jax.named_scope("cross_wait"):
                cross_copy(n, r).wait_recv()
            ps[n, 0, r] = ps[n, 0, r] + d2d[n, r]
            if r == 1:
                for c in far_copies(n):
                    c.start()
            if r == last:
                for c in near_copies(n):
                    c.start()

    def chunk(n, carry):
        with jax.named_scope("down_wait"):
            wait_slot(n)
        with jax.named_scope("down"):
            for e in range(local_experts):
                y = dot(act[e], wbuf[n, e]).astype(BF16)
                for r in range(chips):
                    base = r * pair_cap
                    both = y[base + 32 : base + 48]
                    for q in range(2):
                        row = e * own_cap
                        ybuf[r, q, row : row + 16, :] = y[base + 16 * q : base + 16 * (q + 1)]
                        ybuf[r, q, row + 16 : row + 32, :] = both
        @pl.when(n > 0)
        def _():
            stage1(n - 1)

        with jax.named_scope("combine"):
            for r in far_first:
                for q in (1, 0):
                    parts = dot(a3[r, q], ybuf[r, q])
                    total = parts[0:tokens] + (parts[tokens : 2 * tokens] + parts[2 * tokens : 3 * tokens])
                    for h in range(2):
                        ps[n, q, r, h] = total[:, h * LANES : (h + 1) * LANES]
        for r in far_first:
            cross_copy(n, r).start()
        return carry

    def stage2(n, carry):
        from_left, from_right = far_copies(n)
        to_right, to_left = sum_copies(n)
        from_left.wait_recv()
        ps[n, 0, 1, 0] = ps[n, 0, 1, 0] + far[n, 0]
        to_right.start()
        from_right.wait_recv()
        ps[n, 0, last, 1] = ps[n, 0, last, 1] + far[n, 1]
        to_left.start()
        return carry

    lax.fori_loop(0, chunks, chunk, 0)
    stage1(chunks - 1)
    with jax.named_scope("stage2"):
        lax.fori_loop(0, chunks, stage2, 0)

    def final(n, carry):
        for c in near_copies(n) + sum_copies(n):
            c.wait_recv()
        for h in range(2):
            cols = pl.ds(pl.multiple_of(n * COLS + h * LANES, LANES), LANES)
            total = ps[n, 0, 0, h] + fin[n, 0, h] + fin[n, 1, h]
            out_ref[:, cols] = (x_ref[:, cols].astype(F32) + total).astype(BF16)
        return carry

    with jax.named_scope("final"):
        lax.fori_loop(0, chunks, final, 0)

    def drain(n, carry):
        for r in range(chips):
            cross_copy(n, r).wait_send()
        for c in far_copies(n) + near_copies(n) + sum_copies(n):
            c.wait_send()
        return carry

    lax.fori_loop(0, chunks, drain, 0)
    for c in [c_r0, c_l1, c_r1, c_l0, c_p, f_r, f_l] + list(ids_c.values()) + list(cross.values()):
        c.wait_send()


def solution(mesh):
    group = mesh.shape["ep"]
    chips = group // 2

    def local_block(x_in, norm_gain, w_router, expert_ids, w_gate, w_up, w_down):
        tokens, hidden = x_in.shape
        experts = w_router.shape[1]
        top_k = expert_ids.shape[1]
        local_experts, _, ff = w_gate.shape
        cap = 2 * tokens * top_k // experts
        assert cap == 24 and chips == RING // 2
        chunks = hidden // COLS
        wg = w_gate.reshape(local_experts, 2, hidden // 2, ff)
        wu = w_up.reshape(local_experts, 2, hidden // 2, ff)
        vmem = pl.BlockSpec(memory_space=pltpu.VMEM)
        hbm = pl.BlockSpec(memory_space=pl.ANY)
        dma = pltpu.SemaphoreType.DMA
        return pl.pallas_call(
            moe_kernel,
            out_shape=jax.ShapeDtypeStruct((tokens, hidden), BF16),
            in_specs=[hbm] * 7,
            out_specs=vmem,
            scratch_shapes=[
                pltpu.VMEM((tokens, hidden), BF16),
                pltpu.VMEM((hidden // LANES, LANES), BF16),
                pltpu.VMEM((experts, hidden), BF16),
                pltpu.VMEM((top_k, tokens), jnp.int32),
                pltpu.VMEM((RING, local_experts, ff, COLS), BF16),
                pltpu.VMEM((chips, 2, tokens, hidden), BF16),
                pltpu.VMEM((2, 2 * LANES, hidden), BF16),
                pltpu.VMEM((local_experts, group * cap, hidden), BF16),
                pltpu.VMEM((local_experts, group * cap, ff), BF16),
                pltpu.VMEM((local_experts * 48, 2 * LANES), BF16),
                pltpu.VMEM((chips, 2, local_experts * 32, LANES), F32),
                pltpu.VMEM((chips, 2, 3 * tokens, local_experts * 32), BF16),
                pltpu.VMEM((chips, 2, local_experts * 32, COLS), BF16),
                pltpu.VMEM((chunks, 2, chips, 2, tokens, LANES), F32),
                pltpu.VMEM((chunks, chips, 2, tokens, LANES), F32),
                pltpu.VMEM((chunks, 2, tokens, LANES), F32),
                pltpu.VMEM((chunks, 2, 2, tokens, LANES), F32),
                pltpu.VMEM((chips, 2, top_k, LANES), F32),
                pltpu.VMEM((experts, 2 * LANES), F32),
                pltpu.VMEM((experts, 2 * LANES), F32),
                dma((4,)), dma((RING,)),
                dma((chips, 2)), dma((chips, 2)),
                dma((13,)), dma((chips, 2, 2)),
                dma((chunks, chips)), dma((chunks, chips)),
                dma((chunks, 2)), dma((chunks, 2)),
                dma((chunks, 2, 2)), dma((chunks, 2, 2)),
            ],
            compiler_params=pltpu.CompilerParams(
                collective_id=0, has_side_effects=True, vmem_limit_bytes=67043328
            ),
        )(x_in, norm_gain.reshape(hidden // LANES, LANES), w_router.T, expert_ids.T, wg, wu, w_down)

    tok_spec = P(("dp", "ep"), None)
    expert_spec = P("ep", None, None)
    return jax.shard_map(local_block, mesh=mesh, in_specs=(tok_spec, P(None), P(None, None), tok_spec, expert_spec, expert_spec, expert_spec), out_specs=tok_spec, check_vma=False)
```

time: 85.4 us -> 72.6 us (0.85)
  Pallas kernels: 78.7 us -> 70.7 us
  local copies, waits for them, and re-layouts: 6.39 us -> 1.77 us
    pallas_call x1, Pallas kernels: 78.7 us -> 70.7 us  [local_block(): pl.pallas_call(moe_kernel, out_shape=jax.ShapeDtypeStruct((tokens, hidden...]
    unnamed x3 -> x1, local copies, waits for them, and re-layouts: 5.11 us -> 1.77 us
    reshape x1 -> x0, local copies, waits for them, and re-layouts: 1.28 us -> none  [local_block(): norm_gain.reshape(1, hidden)]
where the time goes in v2:
time: 72.6 us; the launch traced here: 72.5 us
  Pallas kernels  70.7 us (97%)
  local copies, waits for them, and re-layouts  1.77 us (2%)
    pallas_call x1, Pallas kernels, local_block(): pl.pallas_call(moe_kernel, out_shape=jax.ShapeDtypeStruct((tokens, hidden...  70.7 us
    unnamed x1, local copies, waits for them, and re-layouts  1.77 us

profile of v2, /device:TPU:113, one launch (start us, length us, event | category | flops | bytes accessed | tf_op | source)
XLA Modules:
  0.0 72.5 jit_solution(10115109851870291046)
XLA Ops:
  0.0 70.7 %shard_map.73 = bf16[96,2048]{1,0:T(8,128)(2,1)} custom-call(bf16[96,2048]{1,0:T(8,128)(2,1)} %x_hbm.1, bf16[16,128]{1,0:T(8,128)(2,1)} %bitcast.8, bf16[64,2048]{1,0:T(8,128)(2,1)} %bitcast.7, s32[8,96]{1,0:T(8,128)} %bitcast.9, bf16[8,2,1024,1024]{3,2,1,0:T(8,128)(2,1)} %bitcast.5, bf16[8,2,1024,1024]{3,2,1,0:T(8,128)(2,1)} %bitcast.6, ...), custom_call_target="tpu_custom_call" | custom-call | tf_op jit(solution)/shard_map/pallas_call | solution.py:428
  70.7 1.8 %copy.9 = bf16[96,2048]{1,0:T(8,128)(2,1)} copy(bf16[96,2048]{1,0:T(8,128)(2,1)} %shard_map.73) | data formatting | bytes 786432

commit v3 on v2

v3 whole, which is shorter than its diff:
```python
import functools

import jax
import jax.numpy as jnp
from jax import lax
from jax.experimental import pallas as pl
from jax.experimental.pallas import tpu as pltpu
from jax.sharding import PartitionSpec as P

EPS = 1e-6
F32 = jnp.float32
BF16 = jnp.bfloat16
COLS = 256
LANES = 128
RING = 8


def dot(a, b):
    return jnp.dot(a, b, preferred_element_type=F32)


def moe_kernel(
    x_hbm, gain_hbm, wr_hbm, ids_hbm, wg_ref, wu_ref, wd_ref, out_hbm,
    x_ref, gain_ref, wr_ref, ids_ref,
    out_ref, wbuf, xbuf, hbuf, xe, act, oh, gates, a3, ybuf, ps, d2d, far, fin, ids_all, place, soft,
    in_sem, out_sem, wsem, ids_s, ids_r, link_s, cross_s, ag_r, sum_s, d2d_r, far_r, fin_r,
):
    tokens, hidden = x_ref.shape
    local_experts = act.shape[0]
    experts = wr_ref.shape[0]
    chips = xbuf.shape[0]
    half = tokens // 2
    pair_cap = oh.shape[1] // local_experts
    own_cap = 2 * pair_cap // 3
    chunks = hidden // COLS

    me = lax.axis_index("ep")
    chip, core = me // 2, lax.rem(me, 2)

    def device(r, q):
        return {"ep": lax.rem(chip + r, chips) * 2 + (lax.rem(core + q, 2))}

    last = chips - 1
    far_first = (2, 1, last, 0)
    right, left, peer = device(1, 0), device(chips - 1, 0), device(0, 1)

    def remote(src, dst, send, recv, to):
        return pltpu.make_async_remote_copy(
            src_ref=src, dst_ref=dst, send_sem=send, recv_sem=recv,
            device_id=to, device_id_type=pl.DeviceIdType.MESH,
        )

    def start_gate_up(e, parts=range(4)):
        slot = 2 * (e % (RING // 2))
        for n in parts:
            for k, w in enumerate((wg_ref, wu_ref)):
                pltpu.make_async_copy(
                    w.at[e, :, :, pl.ds(n * COLS, COLS)], wbuf.at[slot + k, pl.ds(2 * n, 2)], wsem.at[slot + k]
                ).start()

    def chunk_slot(n):
        return 2 * (n % (RING // 2)) + n // (RING // 2)

    def start_down(n, parts=range(4)):
        for m in parts:
            pltpu.make_async_copy(
                wd_ref.at[pl.ds(2 * m, 2), :, pl.ds(n * COLS, COLS)], wbuf.at[chunk_slot(n), pl.ds(2 * m, 2)], wsem.at[chunk_slot(n)]
            ).start()

    def wait_bytes(ref, sem):
        pltpu.make_async_copy(ref, ref, sem).wait()

    def wait_slot(slot):
        wait_bytes(wbuf.at[slot], wsem.at[slot])

    barrier = pltpu.get_barrier_semaphore()
    others = [(r, q) for r in range(chips) for q in range(2) if (r, q) != (0, 0)]
    for r, q in others:
        pl.semaphore_signal(barrier, inc=1, device_id=device(r, q), device_id_type=pl.DeviceIdType.MESH)
    inputs = [
        pltpu.make_async_copy(a, b, in_sem.at[k])
        for k, (a, b) in enumerate(((ids_hbm, ids_ref), (x_hbm, x_ref), (gain_hbm, gain_ref), (wr_hbm, wr_ref)))
    ]
    for c in inputs:
        c.start()

    ids_all[0, 0] = jnp.full(ids_all.shape[2:], -1.0, F32)
    with jax.named_scope("inputs"):
        for c in inputs:
            c.wait()
    ids_all[0, 0, :, 0:tokens] = ids_ref[...].astype(F32)
    for e in range(RING // 2):
        start_gate_up(e)
    with jax.named_scope("barrier"):
        pl.semaphore_wait(barrier, len(others))

    top, bot = pl.ds(0, half), pl.ds(half, half)
    c_r0 = remote(x_ref.at[top], xbuf.at[last, 0, top], link_s, ag_r.at[0], right)
    c_l1 = remote(x_ref.at[bot], xbuf.at[1, 0, bot], link_s, ag_r.at[1], left)
    c_r1 = remote(x_ref.at[bot], xbuf.at[last, 0, bot], link_s, ag_r.at[2], right)
    c_l0 = remote(x_ref.at[top], xbuf.at[1, 0, top], link_s, ag_r.at[3], left)
    f_r = remote(xbuf.at[last, 0, top], xbuf.at[2, 0, top], link_s, ag_r.at[4], right)
    f_l = remote(xbuf.at[1, 0, bot], xbuf.at[2, 0, bot], link_s, ag_r.at[5], left)
    c_p = remote(x_ref, xbuf.at[0, 1], cross_s, ag_r.at[6], peer)

    def send_ids(r, q):
        back = (chips - r) % chips
        near = int(r == 0)
        remote(ids_all.at[0, 0], ids_all.at[back, q], ids_s.at[near], ids_r.at[near], device(r, q)).start()

    send_ids(0, 1)
    c_p.start()
    for r, q in others:
        if r > 0:
            send_ids(r, q)
    for c in (c_r0, c_l1, c_r1, c_l0):
        c.start()
    cross = {}
    for r, h, k in ((last, 0, 7), (1, 1, 8), (last, 1, 9), (1, 0, 10), (2, 0, 11), (2, 1, 11)):
        rows = (top, bot)[h]
        cross[(r, h)] = remote(xbuf.at[r, 0, rows], xbuf.at[r, 1, rows], cross_s, ag_r.at[k], peer)

    for k in range(hbuf.shape[0]):
        for q in range(2):
            hbuf[k, q * LANES + tokens : (q + 1) * LANES, :] = jnp.zeros((LANES - tokens, hidden), BF16)
    gain = jnp.concatenate([gain_ref[k : k + 1, :] for k in range(gain_ref.shape[0])], axis=1).astype(F32)
    tri = (
        lax.broadcasted_iota(jnp.int32, (LANES, LANES), 0) < lax.broadcasted_iota(jnp.int32, (LANES, LANES), 1)
    ).astype(BF16)

    def norm(src, k, q, h):
        for g in range(half // 16):
            row = h * half + g * 16
            v = src[row : row + 16, :].astype(F32)
            ms = jnp.mean(v * v, axis=-1, keepdims=True)
            hbuf[k, q * LANES + row : q * LANES + row + 16, :] = (v * lax.rsqrt(ms + EPS) * gain).astype(BF16)

    def slots(r):
        first_expert = (me * local_experts).astype(F32)
        eid = lax.broadcasted_iota(jnp.int32, (local_experts, LANES), 0).astype(F32) + first_expert
        rows = []
        for q in range(2):
            ids = ids_all[r, q]
            hit = eid == ids[0:1, :]
            for j in range(1, ids.shape[0]):
                hit = hit | (eid == ids[j : j + 1, :])
            pos = dot(jnp.where(hit, 1.0, 0.0).astype(BF16), tri)
            first = pos < 15.5
            place[r, q] = jnp.where(hit, jnp.where(first, pos, pos + 8.0 * q), -1.0)
            rows.append(jnp.where(hit, jnp.where(first, pos + 16.0 * q, pos + (16.0 + 8.0 * q)), -1.0))
        pair = jnp.concatenate(rows, axis=1)
        slot = lax.broadcasted_iota(jnp.int32, (pair_cap, 2 * LANES), 0).astype(F32)
        for e in range(local_experts):
            oh[r, pl.ds(e * pair_cap, pair_cap), :] = jnp.where(slot == pair[e : e + 1, :], 1.0, 0.0).astype(BF16)

    def gating(r, k):
        logits = lax.dot_general(
            wr_ref[...], hbuf[k], (((1,), (1,)), ((), ())), preferred_element_type=F32
        )
        shifted = jnp.exp(logits - jnp.max(logits, axis=0, keepdims=True))
        prob = shifted / jnp.sum(shifted, axis=0, keepdims=True)
        ids = jnp.concatenate([ids_all[r, 0], ids_all[r, 1]], axis=1)
        eid = lax.broadcasted_iota(jnp.int32, prob.shape, 0).astype(F32)
        chosen = eid == ids[0:1, :]
        for j in range(1, ids.shape[0]):
            chosen = chosen | (eid == ids[j : j + 1, :])
        picked = jnp.where(chosen, prob, 0.0)
        soft[r] = jnp.where(chosen, picked / jnp.sum(picked, axis=0, keepdims=True), 0.0)
        gate = soft[r, pl.ds(pl.multiple_of(me * local_experts, local_experts), local_experts), :]
        slot = lax.broadcasted_iota(jnp.int32, (own_cap, LANES), 0).astype(F32)
        for q in range(2):
            own = place[r, q]
            for e in range(local_experts):
                gates[r, q, pl.ds(e * own_cap, own_cap), :] = jnp.where(
                    slot == own[e : e + 1, :], gate[e : e + 1, q * LANES : (q + 1) * LANES], 0.0
                )

    def gather(r, k):
        for n in range(hidden // COLS):
            cols = slice(n * COLS, (n + 1) * COLS)
            res = dot(oh[r], hbuf[k, :, cols]).astype(BF16)
            for e in range(local_experts):
                xe[e, r * pair_cap : (r + 1) * pair_cap, cols] = res[e * pair_cap : (e + 1) * pair_cap]

    def split_gates(r):
        for q in range(2):
            gt = gates[r, q].T[0:tokens]
            hi = gt.astype(BF16)
            rest = gt - hi.astype(F32)
            mid = rest.astype(BF16)
            low = (rest - mid.astype(F32)).astype(BF16)
            for p, part in enumerate((hi, mid, low)):
                a3[r, q, pl.ds(p * tokens, tokens), :] = part

    own_ids, other_ids = ids_all.at[0, 1], ids_all.at[pl.ds(1, chips - 1)]

    def gate_up_rows(e, rows, after=lambda n: None):
        slot = 2 * (e % (RING // 2))
        data = xe[e, rows, :]
        for n in range(4):
            g = dot(data, wbuf[slot, 2 * n : 2 * n + 2].reshape(hidden, COLS))
            u = dot(data, wbuf[slot + 1, 2 * n : 2 * n + 2].reshape(hidden, COLS))
            act[e, rows, n * COLS : (n + 1) * COLS] = (g * jax.nn.sigmoid(g) * u).astype(BF16)
            after(n)

    own_rows = pl.ds(0, pair_cap)
    rest_rows = pl.ds(pair_cap, (chips - 1) * pair_cap)
    all_rows = pl.ds(0, chips * pair_cap)

    def own_pass(e, carry):
        with jax.named_scope("own_pass"):
            wait_slot(2 * e)
            wait_slot(2 * e + 1)
            gate_up_rows(e, own_rows)
        return carry

    with jax.named_scope("norm_own"):
        norm(x_ref, 0, 0, 0)
        norm(x_ref, 0, 0, 1)
    with jax.named_scope("own_wait"):
        wait_bytes(own_ids, ids_r.at[1])
        c_p.wait_recv()
    with jax.named_scope("prep_own"):
        norm(xbuf.at[0, 1], 0, 1, 0)
        norm(xbuf.at[0, 1], 0, 1, 1)
        slots(0)
        gather(0, 0)
        gating(0, 0)
    lax.fori_loop(0, 1, own_pass, 0)
    with jax.named_scope("slots"):
        wait_bytes(other_ids, ids_r.at[0])
        for r in (last, 1, 2):
            slots(r)
    lax.fori_loop(1, 2, own_pass, 0)
    with jax.named_scope("near_wait"):
        c_r0.wait_recv()
        f_r.start()
        cross[(last, 0)].start()
        c_l1.wait_recv()
        f_l.start()
        cross[(1, 1)].start()
    with jax.named_scope("norm_near"):
        norm(xbuf.at[last, 0], 0, 0, 0)
        norm(xbuf.at[1, 0], 1, 0, 1)
        cross[(last, 0)].wait_recv()
        cross[(1, 1)].wait_recv()
        norm(xbuf.at[last, 1], 0, 1, 0)
        norm(xbuf.at[1, 1], 1, 1, 1)
    lax.fori_loop(2, RING // 2, own_pass, 0)
    with jax.named_scope("near_wait2"):
        c_r1.wait_recv()
        cross[(last, 1)].start()
        c_l0.wait_recv()
        cross[(1, 0)].start()
    with jax.named_scope("norm_near2"):
        norm(xbuf.at[last, 0], 0, 0, 1)
        norm(xbuf.at[1, 0], 1, 0, 0)
        cross[(last, 1)].wait_recv()
        cross[(1, 0)].wait_recv()
        norm(xbuf.at[last, 1], 0, 1, 1)
        norm(xbuf.at[1, 1], 1, 1, 0)
    with jax.named_scope("gather_near"):
        gather(last, 0)
        gather(1, 1)
    with jax.named_scope("far_wait"):
        f_r.wait_recv()
        cross[(2, 0)].start()
        f_l.wait_recv()
        cross[(2, 1)].start()
    with jax.named_scope("gating_near"):
        gating(last, 0)
        gating(1, 1)
    with jax.named_scope("norm_far"):
        norm(xbuf.at[2, 0], 0, 0, 0)
        norm(xbuf.at[2, 0], 0, 0, 1)
    with jax.named_scope("far_cross_wait"):
        wait_bytes(xbuf.at[2, 1], ag_r.at[11])
    with jax.named_scope("norm_far2"):
        norm(xbuf.at[2, 1], 0, 1, 0)
        norm(xbuf.at[2, 1], 0, 1, 1)
    with jax.named_scope("gather_far"):
        gather(2, 0)

    def refill(e):
        def after(n):
            if e < local_experts - RING // 2:
                start_gate_up(e + RING // 2, (n,))
            else:
                start_down(e - (local_experts - RING // 2), (n,))
        return after

    with jax.named_scope("gate_up_rest"):
        for e in range(RING // 2):
            gate_up_rows(e, rest_rows, refill(e))
            if e == 0:
                gating(2, 0)
            split_gates(far_first[chips - 1 - e])
    for e in range(RING // 2, local_experts):
        slot = 2 * (e % (RING // 2))
        with jax.named_scope("gate_up_wait"):
            wait_slot(slot)
            wait_slot(slot + 1)
        with jax.named_scope("gate_up"):
            gate_up_rows(e, all_rows, refill(e))
    for n in range(RING // 2, chunks):
        start_down(n)

    def cross_copy(n):
        return remote(ps.at[n, 1], d2d.at[n], sum_s.at[0], d2d_r.at[n], peer)

    def far_copies(n):
        return (
            remote(ps.at[n, 0, 2, 0], far.at[n, 0], sum_s.at[1], far_r.at[n], right),
            remote(ps.at[n, 0, 2, 1], far.at[n, 1], sum_s.at[1], far_r.at[n], left),
        )

    def near_copies(n):
        return (
            remote(ps.at[n, 0, 1, 1], fin.at[n, 0, 1], sum_s.at[2], fin_r.at[n], right),
            remote(ps.at[n, 0, last, 0], fin.at[n, 1, 0], sum_s.at[2], fin_r.at[n], left),
        )

    def sum_copies(n):
        return (
            remote(ps.at[n, 0, 1, 0], fin.at[n, 0, 0], sum_s.at[2], fin_r.at[n], right),
            remote(ps.at[n, 0, last, 1], fin.at[n, 1, 1], sum_s.at[2], fin_r.at[n], left),
        )

    def stage1(n):
        with jax.named_scope("cross_wait"):
            cross_copy(n).wait_recv()
        for r in far_first:
            ps[n, 0, r] = ps[n, 0, r] + d2d[n, r]
            if r == 1:
                for c in far_copies(n):
                    c.start()
            if r == last:
                for c in near_copies(n):
                    c.start()

    def chunk(n, carry):
        with jax.named_scope("down_wait"):
            wslot = 2 * lax.rem(n, RING // 2) + n // (RING // 2)
            wait_slot(wslot)
        with jax.named_scope("down"):
            for e in range(local_experts):
                y = dot(act[e], wbuf[wslot, e]).astype(BF16)
                for r in range(chips):
                    base = r * pair_cap
                    both = y[base + 32 : base + 48]
                    for q in range(2):
                        row = e * own_cap
                        ybuf[r, q, row : row + 16, :] = y[base + 16 * q : base + 16 * (q + 1)]
                        ybuf[r, q, row + 16 : row + 32, :] = both

        @pl.when(n > 0)
        def _():
            stage1(n - 1)

        with jax.named_scope("combine"):
            for r in far_first:
                for q in (1, 0):
                    parts = dot(a3[r, q], ybuf[r, q])
                    total = parts[0:tokens] + (parts[tokens : 2 * tokens] + parts[2 * tokens : 3 * tokens])
                    for h in range(2):
                        ps[n, q, r, h] = total[:, h * LANES : (h + 1) * LANES]
        cross_copy(n).start()
        return carry

    lax.fori_loop(0, chunks, chunk, 0)
    wait_bytes(act.at[pl.ds(0, 3)], link_s)
    wait_bytes(xbuf.at[pl.ds(0, 2)], cross_s)
    wait_bytes(own_ids, ids_s.at[1])
    wait_bytes(other_ids, ids_s.at[0])
    stage1(chunks - 1)

    def stage2(n, carry):
        to_right, to_left = sum_copies(n)
        with jax.named_scope("far_sum_wait"):
            wait_bytes(far.at[n], far_r.at[n])
        ps[n, 0, 1, 0] = ps[n, 0, 1, 0] + far[n, 0]
        ps[n, 0, last, 1] = ps[n, 0, last, 1] + far[n, 1]
        to_right.start()
        to_left.start()
        return carry

    with jax.named_scope("stage2"):
        lax.fori_loop(0, chunks, stage2, 0)

    def final(n, carry):
        with jax.named_scope("final_wait"):
            wait_bytes(fin.at[n], fin_r.at[n])
        for h in range(2):
            cols = pl.ds(pl.multiple_of(n * COLS + h * LANES, LANES), LANES)
            total = ps[n, 0, 0, h] + fin[n, 0, h] + fin[n, 1, h]
            out_ref[:, cols] = (x_ref[:, cols].astype(F32) + total).astype(BF16)
        cols = pl.ds(pl.multiple_of(n * COLS, COLS), COLS)
        pltpu.make_async_copy(out_ref.at[:, cols], out_hbm.at[:, cols], out_sem).start()
        return carry

    with jax.named_scope("final"):
        lax.fori_loop(0, chunks, final, 0)
    with jax.named_scope("send_wait"):
        wait_bytes(d2d, sum_s.at[0])
        wait_bytes(far, sum_s.at[1])
        wait_bytes(fin, sum_s.at[2])
        wait_bytes(out_ref, out_sem)


def solution(mesh):
    group = mesh.shape["ep"]
    chips = group // 2

    def local_block(x_in, norm_gain, w_router, expert_ids, w_gate, w_up, w_down):
        tokens, hidden = x_in.shape
        experts = w_router.shape[1]
        top_k = expert_ids.shape[1]
        local_experts, _, ff = w_gate.shape
        cap = 2 * tokens * top_k // experts
        assert cap == 24 and chips == RING // 2
        chunks = hidden // COLS
        wg = w_gate.reshape(local_experts, 2, hidden // 2, ff)
        wu = w_up.reshape(local_experts, 2, hidden // 2, ff)
        hbm = pl.BlockSpec(memory_space=pl.ANY)
        dma = pltpu.SemaphoreType.DMA
        return pl.pallas_call(
            moe_kernel,
            out_shape=jax.ShapeDtypeStruct((tokens, hidden), BF16),
            in_specs=[hbm] * 7,
            out_specs=hbm,
            scratch_shapes=[
                pltpu.VMEM((tokens, hidden), BF16),
                pltpu.VMEM((hidden // LANES, LANES), BF16),
                pltpu.VMEM((experts, hidden), BF16),
                pltpu.VMEM((top_k, tokens), jnp.int32),
                pltpu.VMEM((tokens, hidden), BF16),
                pltpu.VMEM((RING, local_experts, ff, COLS), BF16),
                pltpu.VMEM((chips, 2, tokens, hidden), BF16),
                pltpu.VMEM((2, 2 * LANES, hidden), BF16),
                pltpu.VMEM((local_experts, group * cap, hidden), BF16),
                pltpu.VMEM((local_experts, group * cap, ff), BF16),
                pltpu.VMEM((chips, local_experts * 48, 2 * LANES), BF16),
                pltpu.VMEM((chips, 2, local_experts * 32, LANES), F32),
                pltpu.VMEM((chips, 2, 3 * tokens, local_experts * 32), BF16),
                pltpu.VMEM((chips, 2, local_experts * 32, COLS), BF16),
                pltpu.VMEM((chunks, 2, chips, 2, tokens, LANES), F32),
                pltpu.VMEM((chunks, chips, 2, tokens, LANES), F32),
                pltpu.VMEM((chunks, 2, tokens, LANES), F32),
                pltpu.VMEM((chunks, 2, 2, tokens, LANES), F32),
                pltpu.VMEM((chips, 2, top_k, LANES), F32),
                pltpu.VMEM((chips, 2, local_experts, LANES), F32),
                pltpu.VMEM((chips, experts, 2 * LANES), F32),
                dma((4,)), dma, dma((RING,)), dma((2,)), dma((2,)),
                dma, dma, dma((12,)), dma((3,)), dma((chunks,)), dma((chunks,)), dma((chunks,)),
            ],
            compiler_params=pltpu.CompilerParams(
                collective_id=0, has_side_effects=True, vmem_limit_bytes=67043328
            ),
        )(x_in, norm_gain.reshape(hidden // LANES, LANES), w_router.T, expert_ids.T, wg, wu, w_down)

    tok_spec = P(("dp", "ep"), None)
    expert_spec = P("ep", None, None)
    return jax.shard_map(local_block, mesh=mesh, in_specs=(tok_spec, P(None), P(None, None), tok_spec, expert_spec, expert_spec, expert_spec), out_specs=tok_spec, check_vma=False)
```

time: 72.6 us -> 68.8 us (0.948)
  Pallas kernels: 70.7 us -> 66.9 us
    pallas_call x1, Pallas kernels: 70.7 us -> 66.9 us  [local_block(): pl.pallas_call(moe_kernel, out_shape=jax.ShapeDtypeStruct((tokens, hidden...]
where the time goes in v3:
time: 68.8 us; the launch traced here: 68.7 us
  Pallas kernels  66.9 us (97%)
  local copies, waits for them, and re-layouts  1.77 us (3%)
    pallas_call x1, Pallas kernels, local_block(): pl.pallas_call(moe_kernel, out_shape=jax.ShapeDtypeStruct((tokens, hidden...  66.9 us
    unnamed x1, local copies, waits for them, and re-layouts  1.77 us

profile of v3, /device:TPU:113, one launch (start us, length us, event | category | flops | bytes accessed | tf_op | source)
XLA Modules:
  0.0 68.7 jit_solution(11384572923556326862)
XLA Ops:
  0.0 66.9 %shard_map.73 = bf16[96,2048]{1,0:T(8,128)(2,1)} custom-call(bf16[96,2048]{1,0:T(8,128)(2,1)} %x_hbm.1, bf16[16,128]{1,0:T(8,128)(2,1)} %bitcast.8, bf16[64,2048]{1,0:T(8,128)(2,1)} %bitcast.7, s32[8,96]{1,0:T(8,128)} %bitcast.9, bf16[8,2,1024,1024]{3,2,1,0:T(8,128)(2,1)} %bitcast.5, bf16[8,2,1024,1024]{3,2,1,0:T(8,128)(2,1)} %bitcast.6, ...), custom_call_target="tpu_custom_call" | custom-call | tf_op jit(solution)/shard_map/pallas_call | solution.py:426
  66.9 1.8 %copy.9 = bf16[96,2048]{1,0:T(8,128)(2,1)} copy(bf16[96,2048]{1,0:T(8,128)(2,1)} %shard_map.73) | data formatting | bytes 786432

commit v4 on v3

--- a/solution.py
+++ b/solution.py
@@ -22,8 +22,8 @@
 def moe_kernel(
     x_hbm, gain_hbm, wr_hbm, ids_hbm, wg_ref, wu_ref, wd_ref, out_hbm,
     x_ref, gain_ref, wr_ref, ids_ref,
-    out_ref, wbuf, xbuf, hbuf, xe, act, oh, gates, a3, ybuf, ps, d2d, far, fin, ids_all, place, soft,
-    in_sem, out_sem, wsem, ids_s, ids_r, link_s, cross_s, ag_r, sum_s, d2d_r, far_r, fin_r,
+    wbuf, xbuf, hbuf, xe, act, oh, gates, a3, ybuf, ps, d2d, far, fin, ids_all, place, soft,
+    in_sem, wsem, ids_s, ids_r, link_s, cross_s, ag_r, sum_s, d2d_r, far_r, fin_r,
 ):
     tokens, hidden = x_ref.shape
     local_experts = act.shape[0]
@@ -393,9 +393,7 @@
         for h in range(2):
             cols = pl.ds(pl.multiple_of(n * COLS + h * LANES, LANES), LANES)
             total = ps[n, 0, 0, h] + fin[n, 0, h] + fin[n, 1, h]
-            out_ref[:, cols] = (x_ref[:, cols].astype(F32) + total).astype(BF16)
-        cols = pl.ds(pl.multiple_of(n * COLS, COLS), COLS)
-        pltpu.make_async_copy(out_ref.at[:, cols], out_hbm.at[:, cols], out_sem).start()
+            out_hbm[:, cols] = (x_ref[:, cols].astype(F32) + total).astype(BF16)
         return carry
 
     with jax.named_scope("final"):
@@ -404,7 +402,6 @@
         wait_bytes(d2d, sum_s.at[0])
         wait_bytes(far, sum_s.at[1])
         wait_bytes(fin, sum_s.at[2])
-        wait_bytes(out_ref, out_sem)
 
 
 def solution(mesh):
@@ -425,15 +422,14 @@
         dma = pltpu.SemaphoreType.DMA
         return pl.pallas_call(
             moe_kernel,
-            out_shape=jax.ShapeDtypeStruct((tokens, hidden), BF16),
+            out_shape=pltpu.VMEM((tokens, hidden), BF16),
             in_specs=[hbm] * 7,
-            out_specs=hbm,
+            out_specs=pl.BlockSpec(memory_space=pltpu.VMEM),
             scratch_shapes=[
                 pltpu.VMEM((tokens, hidden), BF16),
                 pltpu.VMEM((hidden // LANES, LANES), BF16),
                 pltpu.VMEM((experts, hidden), BF16),
                 pltpu.VMEM((top_k, tokens), jnp.int32),
-                pltpu.VMEM((tokens, hidden), BF16),
                 pltpu.VMEM((RING, local_experts, ff, COLS), BF16),
                 pltpu.VMEM((chips, 2, tokens, hidden), BF16),
                 pltpu.VMEM((2, 2 * LANES, hidden), BF16),
@@ -450,11 +446,11 @@
                 pltpu.VMEM((chips, 2, top_k, LANES), F32),
                 pltpu.VMEM((chips, 2, local_experts, LANES), F32),
                 pltpu.VMEM((chips, experts, 2 * LANES), F32),
-                dma((4,)), dma, dma((RING,)), dma((2,)), dma((2,)),
+                dma((4,)), dma((RING,)), dma((2,)), dma((2,)),
                 dma, dma, dma((12,)), dma((3,)), dma((chunks,)), dma((chunks,)), dma((chunks,)),
             ],
             compiler_params=pltpu.CompilerParams(
-                collective_id=0, has_side_effects=True, vmem_limit_bytes=67043328
+                collective_id=0, has_side_effects=True, vmem_limit_bytes=66600000
             ),
         )(x_in, norm_gain.reshape(hidden // LANES, LANES), w_router.T, expert_ids.T, wg, wu, w_down)
 

time: 68.8 us -> 67.2 us (0.977)
  local copies, waits for them, and re-layouts: 1.77 us -> 0.75 us
    unnamed x1, local copies, waits for them, and re-layouts: 1.77 us -> 0.75 us
where the time goes in v4:
time: 67.2 us; the launch traced here: 67.1 us
  Pallas kernels  66.3 us (99%)
  local copies, waits for them, and re-layouts  0.75 us (1%)
    pallas_call x1, Pallas kernels, local_block(): pl.pallas_call(moe_kernel, out_shape=pltpu.VMEM((tokens, hidden), BF16),...  66.3 us

profile of v4, /device:TPU:113, one launch (start us, length us, event | category | flops | bytes accessed | tf_op | source)
XLA Modules:
  0.0 67.1 jit_solution(7246758125968328314)
XLA Ops:
  0.0 66.3 %shard_map.73 = bf16[96,2048]{1,0:T(8,128)(2,1)S(1)} custom-call(bf16[96,2048]{1,0:T(8,128)(2,1)} %x_hbm.1, bf16[16,128]{1,0:T(8,128)(2,1)} %bitcast.8, bf16[64,2048]{1,0:T(8,128)(2,1)} %bitcast.7, s32[8,96]{1,0:T(8,128)} %bitcast.9, bf16[8,2,1024,1024]{3,2,1,0:T(8,128)(2,1)} %bitcast.5, bf16[8,2,1024,1024]{3,2,1,0:T(8,128)(2,1)} %bitcast.6, ...), custom_call_target="tpu_custom_call" | custom-call | tf_op jit(solution)/shard_map/pallas_call | solution.py:423
  66.3 0.7 %copy.9 = bf16[96,2048]{1,0:T(8,128)(2,1)} copy(bf16[96,2048]{1,0:T(8,128)(2,1)S(1)} %shard_map.73) | data formatting | bytes 786432

commit v5 on v4

--- a/solution.py
+++ b/solution.py
@@ -61,11 +61,9 @@
     def chunk_slot(n):
         return 2 * (n % (RING // 2)) + n // (RING // 2)
 
-    def start_down(n, parts=range(4)):
-        for m in parts:
-            pltpu.make_async_copy(
-                wd_ref.at[pl.ds(2 * m, 2), :, pl.ds(n * COLS, COLS)], wbuf.at[chunk_slot(n), pl.ds(2 * m, 2)], wsem.at[chunk_slot(n)]
-            ).start()
+    def start_down(n):
+        slot = chunk_slot(n)
+        pltpu.make_async_copy(wd_ref.at[:, :, pl.ds(n * COLS, COLS)], wbuf.at[slot], wsem.at[slot]).start()
 
     def wait_bytes(ref, sem):
         pltpu.make_async_copy(ref, ref, sem).wait()
@@ -285,8 +283,8 @@
         def after(n):
             if e < local_experts - RING // 2:
                 start_gate_up(e + RING // 2, (n,))
-            else:
-                start_down(e - (local_experts - RING // 2), (n,))
+            elif n == 3:
+                start_down(e - (local_experts - RING // 2))
         return after
 
     with jax.named_scope("gate_up_rest"):

time: 67.2 us -> 67.2 us (level)
  no operation moved by 1% of the time
where the time goes in v5:
time: 67.2 us; the launch traced here: 67.1 us
  Pallas kernels  66.3 us (99%)
  local copies, waits for them, and re-layouts  0.75 us (1%)
    pallas_call x1, Pallas kernels, local_block(): pl.pallas_call(moe_kernel, out_shape=pltpu.VMEM((tokens, hidden), BF16),...  66.3 us

profile of v5, /device:TPU:113, one launch (start us, length us, event | category | flops | bytes accessed | tf_op | source)
XLA Modules:
  0.0 67.1 jit_solution(11045455646396611817)
XLA Ops:
  0.0 66.3 %shard_map.73 = bf16[96,2048]{1,0:T(8,128)(2,1)S(1)} custom-call(bf16[96,2048]{1,0:T(8,128)(2,1)} %x_hbm.1, bf16[16,128]{1,0:T(8,128)(2,1)} %bitcast.8, bf16[64,2048]{1,0:T(8,128)(2,1)} %bitcast.7, s32[8,96]{1,0:T(8,128)} %bitcast.9, bf16[8,2,1024,1024]{3,2,1,0:T(8,128)(2,1)} %bitcast.5, bf16[8,2,1024,1024]{3,2,1,0:T(8,128)(2,1)} %bitcast.6, ...), custom_call_target="tpu_custom_call" | custom-call | tf_op jit(solution)/shard_map/pallas_call | solution.py:421
  66.3 0.7 %copy.9 = bf16[96,2048]{1,0:T(8,128)(2,1)} copy(bf16[96,2048]{1,0:T(8,128)(2,1)S(1)} %shard_map.73) | data formatting | bytes 786432
